TPU v7x, 16 devices: a whole 2x2x2 slice. The times are simulated.
16 devices in a mesh: dp: 1, tp: 16 (over x, y, z, core).
Axes of the slice: x: 2, y: 2, z: 2, core: 2. Of those that a mesh axis runs over, the one named last changes fastest.
Arguments:
- x: bfloat16 [64, 4608], P('dp')
- k_cache: bfloat16 [64, 4096, 16, 128], P('dp', None, 'tp')
- v_cache: bfloat16 [64, 4096, 16, 128], P('dp', None, 'tp')
- gain_a: bfloat16 [4608], replicated
- wq: bfloat16 [4608, 4096], P(None, 'tp')
- wo: bfloat16 [4096, 4608], P('tp')
- gain_m: bfloat16 [4608], replicated
- w_gate: bfloat16 [4608, 36864], P(None, 'tp')
- w_up: bfloat16 [4608, 36864], P(None, 'tp')
- w_down: bfloat16 [36864, 4608], P('tp')
Outputs:
- output: bfloat16 [64, 4608], P('dp')
All inputs are finite; a program needn't handle non-finite values.
Results may differ from a plain program's by a relative error of at most 0.017.
Values are sent between devices in bfloat16 or wider.
A program may use at most 2 GiB of HBM per device.

v0:
```python
import jax
import jax.numpy as jnp
from jax import lax
from jax.sharding import PartitionSpec as P

HEAD = 128
THETA = 10000


def normed(x, gain):
    wide = x.astype(jnp.float32)
    scale = lax.rsqrt(jnp.mean(wide * wide, -1, keepdims=True) + 1e-6)
    return (wide * scale * gain.astype(jnp.float32)).astype(jnp.bfloat16)


def turned(t, place, theta):
    half = t.shape[-1] // 2
    angle = place.astype(jnp.float32)[:, None] * theta ** (-jnp.arange(half, dtype=jnp.float32) / half)
    cos, sin = jnp.cos(angle)[:, None], jnp.sin(angle)[:, None]
    a, b = t[..., :half].astype(jnp.float32), t[..., half:].astype(jnp.float32)
    return jnp.concatenate([a * cos - b * sin, b * cos + a * sin], -1).astype(jnp.bfloat16)


def matmul(a, w):
    return jnp.dot(a, w, preferred_element_type=jnp.float32).astype(jnp.bfloat16)


def einsum(form, a, b):
    return jnp.einsum(form, a.astype(jnp.float32), b.astype(jnp.float32))


def seen_by(a, wq, k_cache, v_cache, head, theta):
    batch, cache, kv_heads = k_cache.shape[:3]
    place = jnp.full((batch,), cache - 1)
    q = turned(matmul(a, wq).reshape(batch, -1, head), place, theta).reshape(batch, kv_heads, -1, head)
    scores = einsum("bgsd,bugd->bgsu", q, k_cache) * head**-0.5
    weights = jax.nn.softmax(scores, -1).astype(jnp.bfloat16)
    return einsum("bgsu,bugd->bgsd", weights, v_cache).astype(jnp.bfloat16).reshape(batch, -1)


def hidden_of(b, w_gate, w_up):
    gate = jnp.dot(b, w_gate, preferred_element_type=jnp.float32)
    up = jnp.dot(b, w_up, preferred_element_type=jnp.float32)
    return (jax.nn.silu(gate) * up).astype(jnp.bfloat16)


def solution(mesh):
    def added(t, term):
        return (t.astype(jnp.float32) + lax.psum(term.astype(jnp.bfloat16), "tp").astype(jnp.float32)).astype(jnp.bfloat16)

    def step(x, k_cache, v_cache, gain_a, wq, wo, gain_m, w_gate, w_up, w_down):
        seen = seen_by(normed(x, gain_a), wq, k_cache, v_cache, HEAD, THETA)
        h = added(x, jnp.dot(seen, wo, preferred_element_type=jnp.float32))
        return added(h, jnp.dot(hidden_of(normed(h, gain_m), w_gate, w_up), w_down, preferred_element_type=jnp.float32))

    states, cache, columns, rows_of = P("dp", None), P("dp", None, "tp", None), P(None, "tp"), P("tp", None)
    return jax.shard_map(
        step,
        mesh=mesh,
        in_specs=(states, cache, cache, P(None), columns, rows_of, P(None), columns, columns, rows_of),
        out_specs=states,
        check_vma=False,
    )
```

profile of v0, /device:TPU:0, one launch (start us, length us, event | category | flops | bytes accessed | tf_op | source)
XLA Modules:
  0.0 232.3 jit_solution(12812906718037363412)
XLA Ops:
  6.5 0.0 copy-start
  6.5 0.0 all-reduce.3.cloned.1.call-start
  6.6 0.9 convert_element_type.66
  7.5 1.3 fusion.11
  8.7 2.4 %convolution_convert_fusion.2 = bf16[64,256]{1,0:T(8,128)(2,1)S(1)} fusion(bf16[4608,256]{1,0:T(8,128)(2,1)} %param.14, bf16[64,4608]{1,0:T(8,128)(2,1)} %param.10, f32[4608]{0:T(1024)S(1)} %convert_element_type.66, f32[64]{0:T(128)S(1)} %add_rsqrt_fusion.1), kind=kOutput, calls=%fused_computation.28 | convolution fusion | flops 152190976 | bytes 3000576 | tf_op jit(solution)/shard_map/dot_general | solution.py:25
  11.2 0.1 fusion.39
  11.4 0.1 pad_maximum_fusion
  11.5 27.1 %fusion.40 = (f32[64,2]{1,0:T(8,128)S(1)}, f32[64,2,4096]{2,1,0:T(2,128)}) fusion(bf16[64,4096,1,128]{3,1,2,0:T(8,128)(2,1)} %param.11, bf16[64,2,128]{2,0,1:T(8,128)(2,1)S(1)} %pad_maximum_fusion), kind=kOutput, calls=%fused_computation.51 | convolution fusion | flops 135794688 | bytes 69239296 | tf_op jit(solution)/shard_map/sub | solution.py:37
  38.6 23.3 %fusion.19 = bf16[64,2,128]{2,1,0:T(2,128)(2,1)S(1)} fusion(bf16[64,4096,1,128]{3,1,2,0:T(8,128)(2,1)} %param.12, f32[64,2,4096]{2,1,0:T(2,128)} %get-tuple-element.12, f32[64,2]{1,0:T(8,128)S(1)} %get-tuple-element.11), kind=kOutput, calls=%fused_computation.27 | convolution fusion | flops 135282688 | bytes 69239296 | tf_op jit(solution)/shard_map/bgsu,bugd->bgsd/dot_general | solution.py:29
  61.9 0.0 copy-start.3
  61.9 0.0 copy-start.1
  61.9 0.0 copy-done
  61.9 1.4 convolution_convert_fusion.1
  63.3 0.0 all-reduce.3.cloned.1.call-update
  63.3 0.2 all-reduce.5.cloned.1.call-start
  63.6 0.0 copy-done.3
  63.6 0.6 convert_element_type.77
  64.2 68.0 %all-reduce.3.cloned.1.call-done = bf16[64,4608]{1,0:T(8,128)(2,1)} async-done(((bf16[64,4608]{1,0:T(8,128)(2,1)}), bf16[64,4608]{1,0:T(8,128)(2,1)}) %all-reduce.3.cloned.1.call-update) | async-done | bytes 589840 | tf_op jit(solution)/shard_map/psum | solution.py:49
  132.2 0.0 copy-done.1
  132.2 1.4 fusion.15
  133.6 0.0 copy-start.2
  133.6 0.0 slice-start
  133.6 0.0 slice-start.1
  133.6 0.0 slice-start.2
  133.6 9.3 %fusion.27 = f32[64,2304]{1,0:T(8,128)S(1)} fusion(bf16[4608,2304]{1,0:T(8,128)(2,1)} %param.17, bf16[64,4608]{1,0:T(8,128)(2,1)S(1)} %get-tuple-element.6, f32[4608]{0:T(1024)} %convert_element_type.77, f32[64]{0:T(128)S(1)} %add_rsqrt_fusion), kind=kOutput, calls=%fused_computation.32 | convolution fusion | flops 1360134144 | bytes 22432000 | tf_op jit(solution)/shard_map/dot_general | solution.py:42
  142.9 0.0 copy-done.2
  142.9 0.0 slice-start.3
  142.9 0.0 slice-start.4
  142.9 0.0 slice-start.5
  142.9 11.3 %fusion.10 = bf16[64,2304]{1,0:T(8,128)(2,1)S(1)} fusion(bf16[4608,2304]{1,0:T(8,128)(2,1)} %param.18, f32[64,2304]{1,0:T(8,128)S(1)} %fusion.27, bf16[64,4608]{1,0:T(8,128)(2,1)S(1)} %get-tuple-element.6, f32[4608]{0:T(1024)S(1)} %copy-done.2, f32[64]{0:T(128)S(1)} %add_rsqrt_fusion), kind=kOutput, calls=%fused_computation.11 | convolution fusion | flops 1361018880 | bytes 22726912 | tf_op jit(solution)/shard_map/dot_general | solution.py:43
  154.3 0.0 slice-done
  154.3 0.0 slice-done.1
  154.3 0.0 slice-done.2
  154.3 0.0 slice-done.3
  154.3 0.0 slice-done.4
  154.3 0.0 slice-done.5
  154.4 4.6 %convolution_convert_fusion = bf16[64,4608]{1,0:T(8,128)(2,1)} fusion(bf16[64,2304]{1,0:T(8,128)(2,1)S(1)} %fusion.10, bf16[2304,4608]{1,0:T(8,128)(2,1)S(1)} %bitcast.23), kind=kOutput, calls=%fused_computation.5 | convolution fusion | flops 1359249408 | bytes 22118400 | tf_op jit(solution)/shard_map/dot_general | solution.py:54
  159.0 0.0 all-reduce.5.cloned.1.call-update
  159.0 64.5 %all-reduce.5.cloned.1.call-done = bf16[64,4608]{1,0:T(8,128)(2,1)} async-done(((bf16[64,4608]{1,0:T(8,128)(2,1)}), bf16[64,4608]{1,0:T(8,128)(2,1)}) %all-reduce.5.cloned.1.call-update) | async-done | bytes 589840 | tf_op jit(solution)/shard_map/psum | solution.py:49
  223.5 2.0 fusion.18
  (6 shorter events, 0.1 us)
Async XLA Ops:
  6.5 55.4 %copy-start = (bf16[256,4608]{1,0:T(8,128)(2,1)S(1)}, bf16[256,4608]{1,0:T(8,128)(2,1)}, u32[]{:S(2)}) copy-start(bf16[256,4608]{1,0:T(8,128)(2,1)} %param.15) | copy-start | bytes 7077892
  6.5 125.7 %all-reduce.3.cloned.1.call-start = ((), (), s32[]{:S(2)}) async-start(), calls=%async_computation | async-start | bytes 1179648 | tf_op jit(solution)/shard_map/psum | solution.py:49
  61.9 1.6 copy-start.3
  61.9 70.3 %copy-start.1 = (bf16[64,4608]{1,0:T(8,128)(2,1)S(1)}, bf16[64,4608]{1,0:T(8,128)(2,1)}, u32[]{:S(2)}) copy-start(bf16[64,4608]{1,0:T(8,128)(2,1)} %param.10) | copy-start | bytes 1769476
  63.3 160.1 %all-reduce.5.cloned.1.call-start = ((), (), s32[]{:S(2)}) async-start(), calls=%async_computation.1 | async-start | bytes 1179648 | tf_op jit(solution)/shard_map/psum | solution.py:49
  133.6 9.3 %copy-start.2 = (f32[4608]{0:T(1024)S(1)}, f32[4608]{0:T(1024)}, u32[]{:S(2)}) copy-start(f32[4608]{0:T(1024)} %convert_element_type.77) | copy-start | bytes 55300
  133.6 20.7 %slice-start = ((s8[21233664]{0:T(1024)(128)(4,1)}), s8[4194304]{0:T(1024)(128)(4,1)S(1)}, s32[]{:S(2)}) async-start(s8[21233664]{0:T(1024)(128)(4,1)} %bitcast.22), calls=%async_computation.2 | async-start | bytes 8388608
  133.6 20.7 %slice-start.1 = ((s8[21233664]{0:T(1024)(128)(4,1)}), s8[4194304]{0:T(1024)(128)(4,1)S(1)}, s32[]{:S(2)}) async-start(s8[21233664]{0:T(1024)(128)(4,1)} %bitcast.22), calls=%async_computation.3 | async-start | bytes 8388608
  133.6 20.7 %slice-start.2 = ((s8[21233664]{0:T(1024)(128)(4,1)}), s8[4194304]{0:T(1024)(128)(4,1)S(1)}, s32[]{:S(2)}) async-start(s8[21233664]{0:T(1024)(128)(4,1)} %bitcast.22), calls=%async_computation.4 | async-start | bytes 8388608
  142.9 11.4 %slice-start.3 = ((s8[21233664]{0:T(1024)(128)(4,1)}), s8[4194304]{0:T(1024)(128)(4,1)S(1)}, s32[]{:S(2)}) async-start(s8[21233664]{0:T(1024)(128)(4,1)} %bitcast.22), calls=%async_computation.5 | async-start | bytes 8388608
  142.9 11.4 %slice-start.4 = ((s8[21233664]{0:T(1024)(128)(4,1)}), s8[4194304]{0:T(1024)(128)(4,1)S(1)}, s32[]{:S(2)}) async-start(s8[21233664]{0:T(1024)(128)(4,1)} %bitcast.22), calls=%async_computation.6 | async-start | bytes 8388608
  142.9 11.4 %slice-start.5 = ((s8[21233664]{0:T(1024)(128)(4,1)}), s8[262144]{0:T(1024)(128)(4,1)S(1)}, s32[]{:S(2)}) async-start(s8[21233664]{0:T(1024)(128)(4,1)} %bitcast.22), calls=%async_computation.7 | async-start | bytes 524288
Sparse Core Ops, SparseCore 0:
  63.4 68.6 all-reduce.2
  159.1 64.3 all-reduce.4
where the time goes:
time: 233 us; the launch traced here: 232 us
  waiting for transfers between devices  133 us (57%)
  matrix products  79.5 us (34%)
  between operations  13.6 us (6%)
  other arithmetic  6.3 us (3%)
    psum x2, waiting for transfers between devices, added(): lax.psum(term.astype(jnp.bfloat16), 'tp').astype(jnp.float32)  132 us
    sub x1, matrix products, seen_by(): weights = jax.nn.softmax(scores, -1).astype(jnp.bfloat16)  27.1 us
    dot_general x1, matrix products, einsum(): return jnp.einsum(form, a.astype(jnp.float32), b.astype(jnp.float32))  23.3 us
    dot_general x1, matrix products, hidden_of(): up = jnp.dot(b, w_up, preferred_element_type=jnp.float32)  11.3 us
    dot_general x1, matrix products, hidden_of(): gate = jnp.dot(b, w_gate, preferred_element_type=jnp.float32)  9.27 us
  transfers between devices with their start and end apart: 2, of which 2 were waited for; matrix products, arithmetic and copies ran while one was open for 0% of the time, Pallas kernels for 0%

commit v1 on v0

v1 whole, which is shorter than its diff:
```python
import functools

import jax
import jax.numpy as jnp
import numpy as np
from jax import lax
from jax.experimental import pallas as pl
from jax.experimental.pallas import tpu as pltpu
from jax.sharding import PartitionSpec as P

BATCH = 64
CACHE = 4096
D = 4608
HEAD = 128
FFD = 2304
THETA = 10000
N = 16
SLOTS = 24
AHEAD = 4
GROUPS = BATCH // 4
ROWS = 16
UNIT = D // 4
CHUNKS = 3
WIDE = D // CHUNKS
PART = WIDE // 4
KEYS = 512

MESH = pl.DeviceIdType.MESH


def rms(wide, squares, gain):
    return wide * lax.rsqrt(squares / D + 1e-6) * gain


def dot_t(a, b):
    return lax.dot_general(a, b, (((1,), (1,)), ((), ())), preferred_element_type=jnp.float32)


def dot(a, b):
    return jnp.dot(a, b, preferred_element_type=jnp.float32)


def layer(x_ref, ga_ref, gm_ref, cos_ref, sin_ref, k_ref, v_ref, wq_ref, wo_ref, wg_ref, wu_ref, wd_ref, y_ref,
          ring, wo_buf, a_buf, q_buf, o_buf, term, got, h_buf, hid, term2, got2, y_buf,
          ring_sem, wo_sem, y_sem, s1, r1, s2, r2, s3, r3, s4, r4):
    me = lax.axis_index("tp")
    my_row = pl.multiple_of((me // 4) * ROWS, ROWS)
    my_col = me % 4

    def send(src, dst, ss, rs, peer):
        return pltpu.make_async_remote_copy(src_ref=src, dst_ref=dst, send_sem=ss, recv_sem=rs,
                                            device_id={"tp": peer}, device_id_type=MESH)

    def peers(body):
        def one(p, carry):
            body(lax.rem(me + p, N))
            return carry
        lax.fori_loop(1, N, one, 0)

    def cache(g, c):
        slot = lax.rem(g, SLOTS // 4) * 4 + c
        src = k_ref if c < 2 else v_ref
        return [pltpu.make_async_copy(src.at[4 * g + 2 * (c % 2) + i], ring.at[slot, i, pl.ds(0, CACHE)], ring_sem.at[slot, i])
                for i in range(2)]

    def stripe(j):
        slot = lax.rem(j + 16, SLOTS)
        cols = pl.ds(pl.multiple_of(j * 128, 128), 128)
        return [pltpu.make_async_copy(w.at[:, cols], ring.at[slot, i], ring_sem.at[slot, i]) for i, w in enumerate((wg_ref, wu_ref))]

    def down(k):
        slot = k + 10
        return [pltpu.make_async_copy(wd_ref.at[:, pl.ds(pl.multiple_of(k * 512 + c * 128, 128), 128)],
                                      ring.at[slot, c % 2, pl.ds(c // 2 * FFD, FFD)], ring_sem.at[slot, c]) for c in range(4)]

    def start(copies):
        for copy in copies:
            copy.start()

    def wait(copies):
        for copy in copies:
            copy.wait()

    wq_slot = SLOTS - 4
    wq_copies = [pltpu.make_async_copy(wq_ref.at[:, pl.ds(128 * i, 128)], ring.at[wq_slot, i], ring_sem.at[wq_slot, i]) for i in range(2)]
    wo_copy = pltpu.make_async_copy(wo_ref, wo_buf, wo_sem)
    start(wq_copies)
    for g in range(2):
        for c in range(4):
            start(cache(g, c))
    barrier = pltpu.get_barrier_semaphore()
    peers(lambda peer: pl.semaphore_signal(barrier, inc=1, device_id={"tp": peer}, device_id_type=MESH))
    wo_copy.start()
    for g in range(2, AHEAD):
        for c in range(4):
            start(cache(g, c))

    for i in range(4):
        rows = slice(16 * i, 16 * i + 16)
        wide = x_ref[rows, :].astype(jnp.float32)
        a_buf[rows, :] = rms(wide, jnp.sum(wide * wide, -1, keepdims=True), ga_ref[...].astype(jnp.float32)).astype(jnp.bfloat16)
    wait(wq_copies)
    q = dot(a_buf[...], jnp.concatenate([ring[wq_slot, 0], ring[wq_slot, 1]], 1)).astype(jnp.bfloat16).astype(jnp.float32)
    q_rows = jnp.zeros((2 * BATCH, HEAD), jnp.float32)
    row = lax.broadcasted_iota(jnp.int32, (2 * BATCH, BATCH), 0)
    col = lax.broadcasted_iota(jnp.int32, (2 * BATCH, BATCH), 1)
    for head in range(2):
        t = q[:, head * HEAD:(head + 1) * HEAD]
        t = (t * cos_ref[...] + pltpu.roll(t, HEAD // 2, 1) * sin_ref[...]).astype(jnp.bfloat16)
        q_rows += dot(jnp.where(row == 2 * col + head, 1.0, 0.0).astype(jnp.bfloat16), t)
    odd = lax.broadcasted_iota(jnp.int32, (2 * BATCH, HEAD), 0) // 2 % 2
    q_buf[:, :HEAD] = jnp.where(odd == 0, q_rows, 0.0)
    q_buf[:, HEAD:] = jnp.where(odd == 1, q_rows, 0.0)

    def attend(g, carry):
        ahead = g + AHEAD

        @pl.when(ahead < GROUPS)
        def _():
            for c in range(4):
                start(cache(ahead, c))

        @pl.when(ahead >= GROUPS)
        def _():
            for c in range(4):
                start(stripe((ahead - GROUPS) * 4 + c))

        slot = lax.rem(g, SLOTS // 4) * 4
        rows = pl.ds(pl.multiple_of(g * 8, 8), 8)
        first = lax.broadcasted_iota(jnp.int32, (8, 2 * HEAD), 0) < 4
        q8 = q_buf[rows, :]
        qs = [jnp.where(first, q8, 0.0).astype(jnp.bfloat16), jnp.where(first, 0.0, q8).astype(jnp.bfloat16)]
        wait(cache(g, 0))
        wait(cache(g, 1))
        scores = []
        for b in range(CACHE // KEYS):
            keys = slice(b * KEYS, (b + 1) * KEYS)
            s = sum(dot_t(qs[c], jnp.concatenate([ring[slot + c, 0, keys], ring[slot + c, 1, keys]], 1)) for c in range(2))
            scores.append(s * HEAD**-0.5)
        s = jnp.concatenate(scores, 1)
        e = jnp.exp(s - jnp.max(s, -1, keepdims=True))
        w = (e / jnp.sum(e, -1, keepdims=True)).astype(jnp.bfloat16)
        wait(cache(g, 2))
        wait(cache(g, 3))
        outs = [dot(w, jnp.concatenate([ring[slot + 2 + c, 0, :CACHE], ring[slot + 2 + c, 1, :CACHE]], 1)) for c in range(2)]
        out = jnp.where(first, outs[0], outs[1])
        odd8 = lax.broadcasted_iota(jnp.int32, (8, HEAD), 0) // 2 % 2
        o_buf[rows, :] = jnp.where(odd8 == 0, out[:, :HEAD], out[:, HEAD:])
        return carry

    lax.fori_loop(0, GROUPS, attend, 0)
    for j in range(4 * AHEAD, 18):
        start(stripe(j))
    for k in range(6):
        start(down(k))

    seen = [o_buf[pl.ds(head, BATCH, 2), :].astype(jnp.bfloat16) for head in range(2)]
    seen = jnp.concatenate(seen, 1)
    wo_copy.wait()
    for c in range(4):
        t = dot(seen, wo_buf[:, c * UNIT:(c + 1) * UNIT]).astype(jnp.bfloat16)
        for i in range(4):
            term[4 * i + c] = t[16 * i:16 * i + 16]
    pl.semaphore_wait(barrier, N - 1)
    peers(lambda peer: send(term.at[peer], got.at[me], s1.at[peer], r1.at[me], peer).start())
    got[me] = term[me]
    peers(lambda peer: send(term.at[peer], got.at[peer], s1.at[peer], r1.at[peer], peer).wait_recv())
    total = got[0].astype(jnp.float32)
    for p in range(1, N):
        total += got[p].astype(jnp.float32)
    block = (pl.ds(my_row, ROWS), pl.ds(pl.multiple_of(my_col * UNIT, 128), UNIT))
    h_buf[block] = (x_ref[block].astype(jnp.float32) + total).astype(jnp.bfloat16)
    peers(lambda peer: send(h_buf.at[block], h_buf.at[block], s2.at[peer], r2.at[me], peer).start())
    peers(lambda peer: send(h_buf.at[block], h_buf.at[block], s2.at[peer], r2.at[peer], peer).wait_recv())

    for i in range(4):
        rows = slice(16 * i, 16 * i + 16)
        wide = h_buf[rows, :].astype(jnp.float32)
        a_buf[rows, :] = rms(wide, jnp.sum(wide * wide, -1, keepdims=True), gm_ref[...].astype(jnp.float32)).astype(jnp.bfloat16)

    def gate_up(j, carry):
        slot = lax.rem(j + 16, SLOTS)
        wait(stripe(j))
        t = dot(a_buf[...], jnp.concatenate([ring[slot, 0], ring[slot, 1]], 1))
        gate, up = t[:, :128], t[:, 128:]
        hid[:, pl.ds(pl.multiple_of(j * 128, 128), 128)] = (gate * jax.nn.sigmoid(gate) * up).astype(jnp.bfloat16)
        return carry

    lax.fori_loop(0, 3, gate_up, 0)
    for k in range(6, 9):
        start(down(k))
    lax.fori_loop(3, 18, gate_up, 0)

    def out_block(k):
        return pl.ds(my_row, ROWS), pl.ds(pl.multiple_of(k * WIDE + my_col * PART, 128), PART)

    def product(k):
        for t in range(3):
            slot = 3 * k + t + 10
            wait(down(3 * k + t))
            for half in range(2):
                r = slice(half * FFD, (half + 1) * FFD)
                out = dot(hid[...], jnp.concatenate([ring[slot, 0, r], ring[slot, 1, r]], 1)).astype(jnp.bfloat16)
                for s in range(2):
                    piece = 4 * t + 2 * half + s
                    c, off = piece // 3, piece % 3 * 128
                    for i in range(4):
                        term2[k, 4 * i + c, :, off:off + 128] = out[16 * i:16 * i + 16, s * 128:s * 128 + 128]
        peers(lambda peer: send(term2.at[k, peer], got2.at[k, me], s3.at[k, peer], r3.at[k, me], peer).start())

    def finish(k):
        got2[k, me] = term2[k, me]
        peers(lambda peer: send(term2.at[k, peer], got2.at[k, peer], s3.at[k, peer], r3.at[k, peer], peer).wait_recv())
        total = got2[k, 0].astype(jnp.float32)
        for p in range(1, N):
            total += got2[k, p].astype(jnp.float32)
        block = out_block(k)
        y_buf[block] = (h_buf[block].astype(jnp.float32) + total).astype(jnp.bfloat16)
        peers(lambda peer: send(y_buf.at[block], y_buf.at[block], s4.at[k, peer], r4.at[k, me], peer).start())

    def chunk(k, carry):
        product(k)

        @pl.when(k > 0)
        def _():
            finish(k - 1)
        return carry

    lax.fori_loop(0, CHUNKS, chunk, 0)
    finish(CHUNKS - 1)

    def settle(k, carry):
        block = out_block(k)
        peers(lambda peer: send(y_buf.at[block], y_buf.at[block], s4.at[k, peer], r4.at[k, peer], peer).wait_recv())
        return carry

    lax.fori_loop(0, CHUNKS, settle, 0)
    out_copy = pltpu.make_async_copy(y_buf, y_ref, y_sem)
    out_copy.start()

    def sent(peer):
        send(term.at[peer], got.at[me], s1.at[peer], r1.at[me], peer).wait_send()
        block = (pl.ds(my_row, ROWS), pl.ds(pl.multiple_of(my_col * UNIT, 128), UNIT))
        send(h_buf.at[block], h_buf.at[block], s2.at[peer], r2.at[me], peer).wait_send()
        for k in range(CHUNKS):
            send(term2.at[k, peer], got2.at[k, me], s3.at[k, peer], r3.at[k, me], peer).wait_send()
            block = out_block(k)
            send(y_buf.at[block], y_buf.at[block], s4.at[k, peer], r4.at[k, me], peer).wait_send()

    peers(sent)
    out_copy.wait()


def solution(mesh):
    angle = (np.float32(CACHE - 1) * np.float32(THETA) ** (-np.arange(HEAD // 2, dtype=np.float32) / np.float32(HEAD // 2))).astype(np.float32)
    cos, sin = np.cos(angle).astype(np.float32), np.sin(angle).astype(np.float32)
    turn_cos = np.concatenate([cos, cos])[None]
    turn_sin = np.concatenate([-sin, sin])[None]

    def step(x, k_cache, v_cache, gain_a, wq, wo, gain_m, w_gate, w_up, w_down):
        vmem, hbm = pl.BlockSpec(memory_space=pltpu.VMEM), pl.BlockSpec(memory_space=pl.ANY)
        bf, dma = jnp.bfloat16, pltpu.SemaphoreType.DMA
        return pl.pallas_call(
            layer,
            out_shape=jax.ShapeDtypeStruct((BATCH, D), bf),
            in_specs=[vmem] * 5 + [hbm] * 7,
            out_specs=hbm,
            scratch_shapes=[
                pltpu.VMEM((SLOTS, 2, D, 128), bf),
                pltpu.VMEM((2 * HEAD, D), bf),
                pltpu.VMEM((BATCH, D), bf),
                pltpu.VMEM((2 * BATCH, 2 * HEAD), jnp.float32),
                pltpu.VMEM((2 * BATCH, HEAD), jnp.float32),
                pltpu.VMEM((N, ROWS, UNIT), bf),
                pltpu.VMEM((N, ROWS, UNIT), bf),
                pltpu.VMEM((BATCH, D), bf),
                pltpu.VMEM((BATCH, FFD), bf),
                pltpu.VMEM((CHUNKS, N, ROWS, PART), bf),
                pltpu.VMEM((CHUNKS, N, ROWS, PART), bf),
                pltpu.VMEM((BATCH, D), bf),
                dma((SLOTS, 4)), dma(()), dma(()),
                dma((N,)), dma((N,)), dma((N,)), dma((N,)),
                dma((CHUNKS, N)), dma((CHUNKS, N)), dma((CHUNKS, N)), dma((CHUNKS, N)),
            ],
            compiler_params=pltpu.CompilerParams(collective_id=0, has_side_effects=True, vmem_limit_bytes=67_043_328),
        )(x, gain_a[None], gain_m[None], jnp.asarray(turn_cos), jnp.asarray(turn_sin),
          k_cache.reshape(BATCH, CACHE, HEAD), v_cache.reshape(BATCH, CACHE, HEAD), wq, wo, w_gate, w_up, w_down)

    states, cache, columns, rows_of = P("dp", None), P("dp", None, "tp", None), P(None, "tp"), P("tp", None)
    return jax.shard_map(
        step,
        mesh=mesh,
        in_specs=(states, cache, cache, P(None), columns, rows_of, P(None), columns, columns, rows_of),
        out_specs=states,
        check_vma=False,
    )
```

time: 233 us -> 101 us (0.43)
  waiting for transfers between devices: 133 us -> 0 us
  Pallas kernels: 0 us -> 96.1 us
  matrix products: 79.5 us -> 0 us
  between operations: 13.6 us -> 0.01 us
  other arithmetic: 6.3 us -> 0 us
  local copies, waits for them, and re-layouts: 0.18 us -> 4.54 us
    psum x2 -> x0, waiting for transfers between devices: 132 us -> none  [added(): lax.psum(term.astype(jnp.bfloat16), 'tp').astype(jnp.float32)]
    pallas_call x0 -> x1, Pallas kernels: none -> 96.1 us  [step(): pl.pallas_call(layer, out_shape=jax.ShapeDtypeStruct((BATCH, D), bf), in_...]
    dot_general x6 -> x0, matrix products: 52.3 us -> none  [the longest x1 23.3 us: einsum(): return jnp.einsum(form, a.astype(jnp.float32), b.astype(jnp.float32))]
    sub x1 -> x0, matrix products: 27.1 us -> none  [seen_by(): weights = jax.nn.softmax(scores, -1).astype(jnp.bfloat16)]
    convert_element_type x3 -> x0, other arithmetic: 3.47 us -> none  [the longest x1 2.01 us: added(): (t.astype(jnp.float32) + lax.psum(term.astype(jnp.bfloat16), 'tp').astype...]
    reduce_sum x2 -> x0, other arithmetic: 2.65 us -> none  [normed(): scale = lax.rsqrt(jnp.mean(wide * wide, -1, keepdims=True) + 1e-06)]
    broadcast_in_dim x0 -> x2, local copies, waits for them, and re-layouts: none -> 2.63 us  [the longest x1 1.32 us: step(): gain_a[None]]
  transfers between devices with their start and end apart: 2 -> 0, of which waited for: 2 -> 0; matrix products, arithmetic and copies ran while one was open for 0% -> 0% of each run, Pallas kernels for 0% -> 0%
where the time goes in v1:
time: 101 us
  Pallas kernels  96.1 us (95%)
  local copies, waits for them, and re-layouts  4.54 us (4%)
    pallas_call x1, Pallas kernels, step(): pl.pallas_call(layer, out_shape=jax.ShapeDtypeStruct((BATCH, D), bf), in_...  96.1 us

profile of v1, /device:TPU:0, one launch (start us, length us, event | category | flops | bytes accessed | tf_op | source)
XLA Modules:
  0.0 100.7 jit_solution(12167157729756033917)
XLA Ops:
  0.0 1.3 %broadcast_in_dim.6.ga_ref = bf16[1,4608]{1,0:T(2,128)(2,1)} reshape(bf16[4608]{0:T(1024)(128)(2,1)} %param.15) | data formatting | bytes 18432 | tf_op jit(solution)/shard_map/broadcast_in_dim | solution.py:286
  1.3 1.3 %broadcast_in_dim.7.gm_ref = bf16[1,4608]{1,0:T(2,128)(2,1)} reshape(bf16[4608]{0:T(1024)(128)(2,1)} %param.18) | data formatting | bytes 18432 | tf_op jit(solution)/shard_map/broadcast_in_dim | solution.py:286
  2.6 96.1 %shard_map.118 = bf16[64,4608]{1,0:T(8,128)(2,1)} custom-call(bf16[64,4608]{1,0:T(8,128)(2,1)} %x_ref.1, bf16[1,4608]{1,0:T(2,128)(2,1)} %broadcast_in_dim.6.ga_ref, bf16[1,4608]{1,0:T(2,128)(2,1)} %broadcast_in_dim.7.gm_ref, f32[1,128]{1,0:T(1,128)} %constant.4.clone.cos_ref, f32[1,128]{1,0:T(1,128)} %constant.5.clone.sin_ref, ...), custom_call_target="tpu_custom_call" | custom-call | tf_op jit(solution)/shard_map/pallas_call | solution.py:263
  98.8 1.9 %copy.14 = bf16[64,4608]{1,0:T(8,128)(2,1)} copy(bf16[64,4608]{1,0:T(8,128)(2,1)} %shard_map.118) | data formatting | bytes 1179648
